TPU v7x, 128 devices: a whole 4x4x4 slice. The times are simulated.
128 devices in a mesh: dp: 8 (over x, core), vocab: 16 (over y, z).
Axes of the slice: x: 4, y: 4, z: 4, core: 2. Of those that a mesh axis runs over, the one named last changes fastest.
Arguments:
- hidden: bfloat16 [512, 3584], P('dp'), may hold values from -160 to 160
- head_weight: bfloat16 [3584, 152064], P(None, ('dp', 'vocab')), may hold values from -0.3125 to 0.3125
- teacher_ids: int32 [512, 64], P('dp'), may hold values from 0 to 152063, as said below
- teacher_probs: float32 [512, 64], P('dp'), may hold values from 0 to 0.99, as said below
- token_weight: float32 [512], P('dp'), may hold values from 4 to 32
Outputs:
- divergence: float32 [512], P('dp')
- hidden_grad: float32 [512, 3584], P('dp', 'vocab')
Inputs may be any that keep to these rules, and one draw needn't show every extreme that they name: `teacher_ids`: each row names 64 different vocabulary entries. `teacher_probs`: all positive; each row sums to between 0.5 and 0.99.
All inputs are finite; a program needn't handle non-finite values.
Results may differ from a plain program's by a relative error of at most 0.0029.
Values may be sent and summed in bfloat16 or wider, within the bound.
A program may use at most 128 MiB of HBM per device.

v0:
```python
import jax
import jax.numpy as jnp
from jax import lax
from jax.sharding import Mesh
from jax.sharding import PartitionSpec as P

VOCAB = ("vocab_0", "vocab_1")
DP = ("dp_0", "dp_1")
DP_VOCAB = ("dp_0", "dp_1", "vocab_0", "vocab_1")


def side_by_side(arrays, axis, dim, along):
    both = jnp.concatenate(arrays, axis=along)
    out, at, outs = (lax.all_gather(both, axis, axis=dim, tiled=True), 0, [])
    for a in arrays:
        outs.append(lax.slice_in_dim(out, at, at + a.shape[along], axis=along))
        at += a.shape[along]
    return tuple(outs)


def all_in_one(x, axis):
    leaves = jax.tree.leaves(x)
    turns = sorted(range(len(leaves)), key=lambda k: -leaves[k].size)
    width = (1, *leaves[turns[0]].shape)[-1]
    lines = [
        jnp.pad(leaves[k].reshape(-1), (0, -leaves[k].size % width)).reshape(-1, width)
        for k in turns
    ]
    both, at, found = (lax.all_gather(jnp.concatenate(lines), axis), 0, {})
    for k, line in zip(turns, lines):
        piece = both[:, at : at + len(line)].reshape(len(both), -1)
        found[k] = piece[:, : leaves[k].size].reshape(-1, *leaves[k].shape)
        at += len(line)
    numbers = iter(range(len(leaves)))
    return jax.tree.map(lambda _: found[next(numbers)], x)


def combined_by_axis(x, axes, combine):
    for axis in axes:
        pieces = all_in_one(x, axis)
        x = jax.tree.map(lambda part: part[0], pieces)
        for k in range(1, lax.axis_size(axis)):
            x = combine(x, jax.tree.map(lambda part: part[k], pieces))
    return x


def split_up(x, dim, length):
    dims = x.shape
    pieces = x.reshape(*dims[:dim], length, dims[dim] // length, *dims[dim + 1 :])
    return jnp.moveaxis(pieces, dim, 0)


def sent_and_summed(x, axis, dim):
    length = lax.axis_size(axis)
    pieces = lax.all_to_all(split_up(x, dim, length), axis, 0, 0, tiled=True)
    return jnp.sum(pieces, axis=0)


def combine_parts(first, second):
    largest = jnp.maximum(first[0], second[0])
    scaled = first[1] * jnp.exp(first[0] - largest) + second[1] * jnp.exp(second[0] - largest)
    return (largest, scaled, first[2] + second[2])


def body(hidden, head_weight, teacher_ids, teacher_probs, token_weight):
    tok_rows = hidden.shape[0]
    local_cols = head_weight.shape[1]
    vocab_count = lax.axis_size(VOCAB)
    offset = (lax.axis_index(DP) * vocab_count + lax.axis_index(VOCAB)) * local_cols
    logits = jnp.dot(
        lax.all_gather(hidden, DP, axis=0, tiled=True),
        head_weight,
        preferred_element_type=jnp.float32,
    )
    all_rows = logits.shape[0]
    id_values, probs = side_by_side((teacher_ids.astype(jnp.float32), teacher_probs), DP, 0, 1)
    local_ids = id_values.astype(jnp.int32) - offset
    top_count = local_ids.shape[1]
    group_size = 8
    columns = lax.broadcasted_iota(jnp.int32, (1, 1, local_cols), 2)

    def add_group(index, sparse_now):
        ids_part = lax.dynamic_slice_in_dim(local_ids, index * group_size, group_size, 1)
        probs_part = lax.dynamic_slice_in_dim(probs, index * group_size, group_size, 1)
        matches = ids_part[:, :, None] == columns
        return sparse_now + jnp.sum(jnp.where(matches, probs_part[:, :, None], 0.0), axis=1)

    sparse = lax.fori_loop(
        0, top_count // group_size, add_group, jnp.zeros((all_rows, local_cols), jnp.float32)
    )
    picked = jnp.sum(sparse * logits, axis=1)
    local_peak = jnp.max(logits, axis=1)
    local_sum = jnp.sum(jnp.exp(logits - local_peak[:, None]), axis=1)
    largest, expsum, weighted = combined_by_axis(
        (local_peak, local_sum, picked), DP_VOCAB, combine_parts
    )
    log_norm = largest + jnp.log(expsum)
    mass = jnp.sum(probs, axis=1)
    divergence_all = jnp.sum(probs * jnp.log(probs), axis=1) - weighted + mass * log_norm
    divergence = lax.dynamic_slice_in_dim(
        divergence_all, lax.axis_index(DP) * tok_rows, tok_rows, 0
    )
    logit_grad = (mass[:, None] * jnp.exp(logits - log_norm[:, None]) - sparse).astype(jnp.bfloat16)
    row_sums = lax.psum_scatter(
        lax.dot_general(
            logit_grad, head_weight, (((1,), (1,)), ((), ())), preferred_element_type=jnp.float32
        ),
        DP,
        scatter_dimension=0,
        tiled=True,
    )
    summed = sent_and_summed(row_sums, VOCAB, 1)
    return (divergence, token_weight[:, None] * summed)


def solution(mesh):
    split = Mesh(mesh.devices.reshape(4, 2, 4, 4), ("dp_0", "dp_1", "vocab_0", "vocab_1"))
    placed = (P(DP, None), P(None, DP_VOCAB), P(DP, None), P(DP, None), P(DP))
    return jax.shard_map(
        body, mesh=split, in_specs=placed, out_specs=(P(DP), P(DP, VOCAB)), check_vma=False
    )
```

profile of v0, /device:TPU:0, one launch (start us, length us, event | category | flops | bytes accessed | tf_op | source)
XLA Modules:
  0.0 303.8 jit_solution(13453206169107148406)
XLA Ops:
  7.2 0.0 all-gather.10.cloned.1.call-start
  7.2 0.7 all-gather.10.cloned.1.call-update
  7.9 0.0 reduce-scatter.2.cloned.1.call-start
  8.0 0.8 convert_element_type.9
  8.7 0.8 pad_maximum_fusion
  9.6 13.3 %all_gather.30 = f32[512,128]{1,0:T(8,128)S(1)} all-gather(f32[64,128]{1,0:T(8,128)S(1)} %pad_maximum_fusion), channel_id=1, replica_groups=mesh['dp_0'=4,'dp_1'=2,'vocab_0'=4,'vocab_1'=4] {'dp_0','dp_1'}, dimensions={0}, use_global_device_ids=true | all-gather | bytes 294912 | tf_op jit(solution)/shard_map/all_gather | solution.py:14
  22.8 0.3 fusion.5
  23.2 0.1 copy.15
  23.3 0.1 copy.16
  23.4 138.3 %while.14 = (s32[]{:T(128)}, f32[512,1188]{0,1:T(8,128)S(1)}, s32[512,64]{0,1:T(8,128)S(1)}, f32[512,64]{0,1:T(8,128)S(1)}, s32[]{:T(128)}, /*index=5*/s32[]{:T(128)}, s32[]{:T(128)}, s32[]{:T(128)}) while((s32[]{:T(128)}, f32[512,1188]{0,1:T(8,128)S(1)}, s32[512,64]{0,1:T(8,128)S(1)}, f32[512,64]{0,1:T(8,128)S(1)}, s32[]{:T(128)}, ...), condition=%wide.region_5.6_spmd.clone, body=%wide.region_3.0_spmd.clone.sunk | while | flops 15206407 | bytes 9830557 | solution.py:88
  23.5 16.4 %select_reduce_fusion.2 = f32[512,1188]{0,1:T(8,128)S(1)} fusion(f32[512,8]{0,1:T(8,128)S(1)} %constant_dynamic-slice_fusion.4, s32[512,8]{0,1:T(8,128)S(1)} %constant_dynamic-slice_fusion.5), kind=kLoop, calls=%fused_computation.2.clone.1 | loop fusion | flops 13989888 | bytes 2465792 | tf_op jit(solution)/shard_map/while/body/eval_jaxpr/reduce_sum | solution.py:86
  39.9 0.8 select_add_fusion.2
  40.8 16.4 %select_reduce_fusion.2 = f32[512,1188]{0,1:T(8,128)S(1)} fusion(f32[512,8]{0,1:T(8,128)S(1)} %constant_dynamic-slice_fusion.4, s32[512,8]{0,1:T(8,128)S(1)} %constant_dynamic-slice_fusion.5), kind=kLoop, calls=%fused_computation.2.clone.1 | loop fusion | flops 13989888 | bytes 2465792 | tf_op jit(solution)/shard_map/while/body/eval_jaxpr/reduce_sum | solution.py:86
  57.2 0.8 select_add_fusion.2
  58.1 16.4 %select_reduce_fusion.2 = f32[512,1188]{0,1:T(8,128)S(1)} fusion(f32[512,8]{0,1:T(8,128)S(1)} %constant_dynamic-slice_fusion.4, s32[512,8]{0,1:T(8,128)S(1)} %constant_dynamic-slice_fusion.5), kind=kLoop, calls=%fused_computation.2.clone.1 | loop fusion | flops 13989888 | bytes 2465792 | tf_op jit(solution)/shard_map/while/body/eval_jaxpr/reduce_sum | solution.py:86
  74.5 0.8 select_add_fusion.2
  75.4 16.4 %select_reduce_fusion.2 = f32[512,1188]{0,1:T(8,128)S(1)} fusion(f32[512,8]{0,1:T(8,128)S(1)} %constant_dynamic-slice_fusion.4, s32[512,8]{0,1:T(8,128)S(1)} %constant_dynamic-slice_fusion.5), kind=kLoop, calls=%fused_computation.2.clone.1 | loop fusion | flops 13989888 | bytes 2465792 | tf_op jit(solution)/shard_map/while/body/eval_jaxpr/reduce_sum | solution.py:86
  91.8 0.8 select_add_fusion.2
  92.7 16.4 %select_reduce_fusion.2 = f32[512,1188]{0,1:T(8,128)S(1)} fusion(f32[512,8]{0,1:T(8,128)S(1)} %constant_dynamic-slice_fusion.4, s32[512,8]{0,1:T(8,128)S(1)} %constant_dynamic-slice_fusion.5), kind=kLoop, calls=%fused_computation.2.clone.1 | loop fusion | flops 13989888 | bytes 2465792 | tf_op jit(solution)/shard_map/while/body/eval_jaxpr/reduce_sum | solution.py:86
  109.1 0.8 select_add_fusion.2
  110.0 16.4 %select_reduce_fusion.2 = f32[512,1188]{0,1:T(8,128)S(1)} fusion(f32[512,8]{0,1:T(8,128)S(1)} %constant_dynamic-slice_fusion.4, s32[512,8]{0,1:T(8,128)S(1)} %constant_dynamic-slice_fusion.5), kind=kLoop, calls=%fused_computation.2.clone.1 | loop fusion | flops 13989888 | bytes 2465792 | tf_op jit(solution)/shard_map/while/body/eval_jaxpr/reduce_sum | solution.py:86
  126.3 0.8 select_add_fusion.2
  127.3 16.4 %select_reduce_fusion.2 = f32[512,1188]{0,1:T(8,128)S(1)} fusion(f32[512,8]{0,1:T(8,128)S(1)} %constant_dynamic-slice_fusion.4, s32[512,8]{0,1:T(8,128)S(1)} %constant_dynamic-slice_fusion.5), kind=kLoop, calls=%fused_computation.2.clone.1 | loop fusion | flops 13989888 | bytes 2465792 | tf_op jit(solution)/shard_map/while/body/eval_jaxpr/reduce_sum | solution.py:86
  143.6 0.8 select_add_fusion.2
  144.5 16.4 %select_reduce_fusion.2 = f32[512,1188]{0,1:T(8,128)S(1)} fusion(f32[512,8]{0,1:T(8,128)S(1)} %constant_dynamic-slice_fusion.4, s32[512,8]{0,1:T(8,128)S(1)} %constant_dynamic-slice_fusion.5), kind=kLoop, calls=%fused_computation.2.clone.1 | loop fusion | flops 13989888 | bytes 2465792 | tf_op jit(solution)/shard_map/while/body/eval_jaxpr/reduce_sum | solution.py:86
  160.9 0.8 select_add_fusion.2
  161.8 0.0 all-gather.10.cloned.1.call-done
  161.8 8.3 %fusion.48 = (f32[512]{0:T(512)S(1)}, f32[512,1188]{0,1:T(8,128)S(1)}) fusion(bf16[512,3584]{1,0:T(8,128)(2,1)} %all-gather.10.cloned.1.call-done, bf16[3584,1188]{0,1:T(8,128)(2,1)} %param.8), kind=kOutput, calls=%fused_computation.97 | convolution fusion | flops 4360586752 | bytes 14620672 | tf_op jit(solution)/shard_map/dot_general | solution.py:70
  170.1 0.7 exponential_reduce_fusion
  170.8 11.9 %all-gather.4 = f32[4,3,512]{2,1,0:T(4,128)S(1)} all-gather(f32[1,3,512]{2,1,0:T(4,128)S(1)} %maximum_bitcast_fusion), channel_id=2, replica_groups=mesh['dp_0'=4,'dp_1'=2,'vocab_0'=4,'vocab_1'=4] {'dp_0'}, dimensions={0}, use_global_device_ids=true | all-gather | bytes 30720 | tf_op jit(solution)/shard_map/all_gather | solution.py:29
  182.8 1.8 all-gather.5
  184.7 12.4 %all-gather.6 = f32[4,3,512]{2,1,0:T(4,128)S(1)} all-gather(f32[1,3,512]{2,1,0:T(4,128)S(1)} %maximum_bitcast_fusion.2), channel_id=4, replica_groups=mesh['dp_0'=4,'dp_1'=2,'vocab_0'=4,'vocab_1'=4] {'vocab_0'}, dimensions={0}, use_global_device_ids=true | all-gather | bytes 30720 | tf_op jit(solution)/shard_map/all_gather | solution.py:29
  197.2 13.3 %all-gather.7 = f32[4,3,512]{2,1,0:T(4,128)S(1)} all-gather(f32[1,3,512]{2,1,0:T(4,128)S(1)} %maximum_bitcast_fusion.3), channel_id=5, replica_groups=mesh['dp_0'=4,'dp_1'=2,'vocab_0'=4,'vocab_1'=4] {'vocab_1'}, dimensions={0}, use_global_device_ids=true | all-gather | bytes 30720 | tf_op jit(solution)/shard_map/all_gather | solution.py:29
  210.6 10.7 %fusion.2 = f32[512,3584]{1,0:T(8,128)} fusion(bf16[3584,1188]{0,1:T(8,128)(2,1)} %param.8, f32[512,1188]{0,1:T(8,128)S(1)} %get-tuple-element.96, f32[512,1188]{0,1:T(8,128)S(1)} %get-tuple-element.149, f32[512]{0:T(512)S(1)} %get-tuple-element.131, f32[512]{0:T(512)S(1)} %get-tuple-element.121), kind=kOutput, calls=%fused_computation.9 | convolution fusion | flops 4362412032 | bytes 20725760 | tf_op jit(solution)/shard_map/dot_general | solution.py:105
  221.2 0.0 reduce-scatter.2.cloned.1.call-update
  221.3 47.5 %reduce-scatter.2.cloned.1.call-done = f32[64,3584]{1,0:T(8,128)} async-done(((f32[512,3584]{1,0:T(8,128)}), f32[64,3584]{1,0:T(8,128)}) %reduce-scatter.2.cloned.1.call-update) | async-done | bytes 917520 | tf_op jit(solution)/shard_map/reduce_scatter | solution.py:104
  268.7 1.8 reshape.708
  270.6 0.0 copy-start
  270.6 1.6 copy.19
  272.2 7.0 %all-to-all-start = ((f32[16,64,224]{2,1,0:T(8,128)}), f32[16,64,224]{2,1,0:T(8,128)S(1)}, u32[]{:S(2)}, u32[]{:S(2)}) async-start(f32[16,64,224]{2,1,0:T(8,128)} %bitcast.201), calls=%async_computation.1 | async-start | bytes 2097152 | tf_op jit(solution)/shard_map/all_to_all | solution.py:55
  279.2 0.6 dynamic_slice.17
  279.8 16.4 %all-to-all-done = f32[16,64,224]{2,1,0:T(8,128)S(1)} async-done(((f32[16,64,224]{2,1,0:T(8,128)}), f32[16,64,224]{2,1,0:T(8,128)S(1)}, u32[]{:S(2)}, u32[]{:S(2)}) %all-to-all-start) | async-done | bytes 917536 | tf_op jit(solution)/shard_map/all_to_all | solution.py:55
  296.2 0.1 reduce_sum.62
  296.2 0.0 copy-done
  296.2 0.7 broadcast_multiply_fusion
  (30 shorter events, 0.4 us)
Async XLA Ops:
  7.2 154.6 %all-gather.10.cloned.1.call-start = ((), (), s32[]{:S(2)}) async-start(), calls=%async_computation.2 | async-start | bytes 4128768 | tf_op jit(solution)/shard_map/all_gather | solution.py:71
  7.9 260.8 %reduce-scatter.2.cloned.1.call-start = ((), (), s32[]{:S(2)}) async-start(), calls=%async_computation.3 | async-start | bytes 8257536 | tf_op jit(solution)/shard_map/reduce_scatter | solution.py:104
  270.6 25.7 %copy-start = (f32[64]{0:T(128)S(1)}, f32[64]{0:T(128)}, u32[]{:S(2)}) copy-start(f32[64]{0:T(128)} %param.11) | copy-start | bytes 772
  272.2 24.0 %all-to-all-start = ((f32[16,64,224]{2,1,0:T(8,128)}), f32[16,64,224]{2,1,0:T(8,128)S(1)}, u32[]{:S(2)}, u32[]{:S(2)}) async-start(f32[16,64,224]{2,1,0:T(8,128)} %bitcast.201), calls=%async_computation.1 | async-start | bytes 2097152 | tf_op jit(solution)/shard_map/all_to_all | solution.py:55
Sparse Core Ops, SparseCore 0:
  9.7 32.3 all-gather.9
  221.4 47.3 reduce-scatter.1
where the time goes:
time: 305 us; the launch traced here: 304 us
  other arithmetic  141 us (46%)
  waiting for transfers between devices  64.6 us (21%)
  blocking collectives  52.8 us (17%)
  matrix products  19 us (6%)
  between operations  14.2 us (5%)
  starting transfers between devices  7.04 us (2%)
  local copies, waits for them, and re-layouts  4.42 us (1%)
    reduce_sum x8, other arithmetic, add_group(): jnp.sum(jnp.where(matches, probs_part[:, :, None], 0.0), axis=1)  131 us
    reduce_scatter x1, waiting for transfers between devices, body(): lax.psum_scatter(lax.dot_general(logit_grad, head_weight, (((1,), (1,)),...  47.5 us
    all_gather x4, blocking collectives, all_in_one(): both, at, found = (lax.all_gather(jnp.concatenate(lines), axis), 0, {})  39.5 us
    all_to_all x1, waiting for transfers between devices, sent_and_summed(): pieces = lax.all_to_all(split_up(x, dim, length), axis, 0, 0, tiled=True)  16.4 us
    all_gather x1, blocking collectives, side_by_side(): out, at, outs = (lax.all_gather(both, axis, axis=dim, tiled=True), 0, [])  13.3 us
    dot_general x1, matrix products, body(): lax.dot_general(logit_grad, head_weight, (((1,), (1,)), ((), ())), prefer...  10.7 us
    dot_general x1, matrix products, body(): jnp.dot(lax.all_gather(hidden, DP, axis=0, tiled=True), head_weight, pref...  8.29 us
    all_to_all x1, starting transfers between devices, sent_and_summed(): pieces = lax.all_to_all(split_up(x, dim, length), axis, 0, 0, tiled=True)  6.96 us
  transfers between devices with their start and end apart: 3, of which 2 were waited for; matrix products, arithmetic and copies ran while one was open for 46% of the time, Pallas kernels for 0%

commit v1 on v0

v1 whole, which is shorter than its diff:
```python
import functools

import jax
import jax.numpy as jnp
from jax import lax
from jax.experimental import pallas as pl
from jax.experimental.pallas import tpu as pltpu
from jax.sharding import Mesh
from jax.sharding import PartitionSpec as P

MESH = pl.DeviceIdType.MESH
DP = ("x", "c")
VOCAB = ("y", "z")
F32 = jnp.float32
BF16 = jnp.bfloat16
COLOURS = (
    (("x", "y", "z"), ((0, 16), (0, 8))),
    (("y", "z", "x"), ((16, 8), (8, 16))),
    (("z", "x", "y"), ((24, 8), (24, 8))),
)
WIRE2 = F32


def kernel(h, w, ids, pr, tw, out, dv, *scratch, names):
    S = dict(zip(names, scratch))
    D = h.shape[1]
    C = w.shape[1]
    TOP = ids.shape[1]
    Z = D // 16
    co = {a: lax.axis_index(a) for a in ("x", "c", "y", "z")}
    x, c, y, z = co["x"], co["c"], co["y"], co["z"]
    oc = 1 - c
    count = [0]

    def step(axis, d):
        return lax.rem(co[axis] + d, 4)

    def send(src, dst, **dev):
        i = count[0]
        count[0] += 1
        cp = pltpu.make_async_remote_copy(
            src_ref=src, dst_ref=dst, send_sem=S["ss"].at[i], recv_sem=S["rs"].at[i],
            device_id=dev, device_id_type=MESH,
        )
        cp.start()
        sent.append(cp)
        return cp

    sent = []
    wcopy = pltpu.make_async_copy(w, S["W"], S["ws"])
    wcopy.start()
    H, IP, W = S["H"], S["IP"], S["W"]
    me = c * 4 + x
    IP[me, :, 0:TOP] = pr[...]
    IP[me, :, TOP : 2 * TOP] = ids[...].astype(F32)
    for r in range(2):
        H[r, pl.ds(pl.multiple_of(me * 32, 32), 32), :] = h[r * 32 : r * 32 + 32, :]

    bar = pltpu.get_barrier_semaphore()
    for d in range(4):
        for e in range(2):
            if d or e:
                pl.semaphore_signal(
                    bar, inc=1, device_id={"x": step("x", d), "c": lax.rem(c + e, 2)}, device_id_type=MESH
                )
    for d in range(4):
        for e in range(4):
            if d or e:
                pl.semaphore_signal(
                    bar, inc=1, device_id={"y": step("y", d), "z": step("z", e)}, device_id_type=MESH
                )
    pl.semaphore_wait(bar, 22)

    share = (lax.rem(y + 2 * z, 4), lax.rem(2 * y + z, 4))
    X, Pn, Cn, In, Ic = [{}, {}], [{}, {}], [{}, {}], {}, {}

    def hrows(r, core, xb, off, n):
        return H.at[r, pl.ds(pl.multiple_of(core * 128 + xb * 32 + off, 8), n), :]

    def send_x(r):
        for d in (1, 3, 2):
            src = h.at[pl.ds(pl.multiple_of(r * 32 + share[r] * 8, 8), 8), :]
            X[r][d] = send(src, hrows(r, c, x, share[r] * 8, 8), x=step("x", d))
        Cn[r][0] = send(h.at[pl.ds(r * 32, 32), :], hrows(r, c, x, 0, 32), c=oc)

    def forward(r):
        full, half = (("y", "z"), ("z", "y"))[r]
        for d in (1, 3, 2):
            X[r][d].wait_recv()
            xs = step("x", 4 - d)
            rows = pl.ds(pl.multiple_of(c * 128 + xs * 32 + share[r] * 8, 8), 8)
            whole = H.at[r, rows, :]
            lo, hi = H.at[r, rows, 0 : D // 2], H.at[r, rows, D // 2 : D]
            Pn[r][d] = [
                send(whole, whole, **{full: step(full, 1)}),
                send(whole, whole, **{full: step(full, 3)}),
                send(lo, lo, **{half: step(half, 1)}),
                send(hi, hi, **{half: step(half, 3)}),
            ]

    def to_sibling(r):
        for d in (1, 3, 2):
            for cp in Pn[r][d]:
                cp.wait_recv()
            xs = step("x", 4 - d)
            blk = hrows(r, c, xs, 0, 32)
            Cn[r][d] = send(blk, blk, c=oc)

    send_x(0)
    for d in (1, 3, 2):
        In[d] = send(IP.at[me], IP.at[me], x=step("x", d))
    Ic[0] = send(IP.at[me], IP.at[me], c=oc)
    send_x(1)
    forward(0)
    for d in (1, 3, 2):
        In[d].wait_recv()
        s = c * 4 + step("x", 4 - d)
        Ic[d] = send(IP.at[s], IP.at[s], c=oc)
    forward(1)
    to_sibling(0)
    for d in range(4):
        Ic[d].wait_recv()

    dp_index = x * 2 + c
    offset = (dp_index * 16 + y * 4 + z) * C
    SP = S["SP"]

    def sparse(r, lo, hi):
        def group(g, _):
            blk = g // 2
            j0 = r * 32 + (g % 2) * 16
            rows = pl.ds(pl.multiple_of(j0, 16), 16)
            local = IP[blk, rows, TOP : 2 * TOP].astype(jnp.int32) - offset
            local = jnp.where((local >= 0) & (local < C), local, -1).astype(jnp.int16)
            lane = lax.broadcasted_iota(jnp.int32, (16, 128), 1)
            n = -(-C // 128)
            cols = [(lane + 128 * k).astype(jnp.int16) for k in range(n)]
            acc = [jnp.full((16, 128), 127, jnp.int16) for _ in range(n)]
            for k in range(TOP):
                one = jnp.broadcast_to(local[:, k : k + 1], (16, 128))
                for j in range(n):
                    acc[j] = jnp.where(one == cols[j], jnp.int16(k), acc[j])
            for j in range(n):
                which = acc[j].astype(jnp.int32)
                wide = min(128, C - 128 * j)
                for s in range(2):
                    table = IP[blk, pl.ds(pl.multiple_of(j0 + s * 8, 8), 8), :]
                    sel = which[s * 8 : s * 8 + 8]
                    got = jnp.where(sel < TOP, jnp.take_along_axis(table, sel, axis=1), 0.0)
                    SP[r, pl.ds(pl.multiple_of(g * 16 + s * 8, 8), 8), 128 * j : 128 * j + wide] = got[:, :wide]
            return 0

        lax.fori_loop(lo, hi, group, 0)

    eye = (
        lax.broadcasted_iota(jnp.int32, (128, 128), 0) == lax.broadcasted_iota(jnp.int32, (128, 128), 1)
    )

    def to_row(col):
        return jnp.sum(jnp.where(eye, jnp.broadcast_to(col, (128, 128)), 0.0), axis=0, keepdims=True)

    def to_col(row):
        return jnp.sum(jnp.where(eye, jnp.broadcast_to(row, (128, 128)), 0.0), axis=1, keepdims=True)

    L, ST = S["L"], S["ST"]
    SA, SB = S["SA"], S["SB"]

    def spread(buf, r, slot, near):
        ref = buf.at[r, slot]
        if near:
            return [
                send(ref, ref, x=step("x", d), c=lax.rem(c + e, 2))
                for d in range(4) for e in range(2) if d or e
            ]
        return [
            send(ref, ref, y=step("y", d), z=step("z", e))
            for d in range(4) for e in range(4) if d or e
        ]

    def first_dot(r):
        L[r] = jnp.dot(H[r], W[...], preferred_element_type=F32)

    def stats(r):
        def part(i, _):
            rows = pl.ds(pl.multiple_of(i * 32, 32), 32)
            v = L[r, rows, :]
            m = jnp.max(v, axis=1, keepdims=True)
            ST[rows, 0:1] = m
            ST[rows, 1:2] = jnp.sum(jnp.exp(v - m), axis=1, keepdims=True)
            return 0

        lax.fori_loop(0, 8, part, 0)
        for b in range(2):
            SA[r, me, b : b + 1, :] = to_row(ST[b * 128 : b * 128 + 128, 0:1])
            SA[r, me, b + 2 : b + 3, :] = to_row(ST[b * 128 : b * 128 + 128, 1:2])
        return spread(SA, r, me, True)

    def merged(buf, r, n, copies):
        for cp in copies:
            cp.wait_recv()
        m = buf[r, 0, 0:2, :]
        for k in range(1, n):
            m = jnp.maximum(m, buf[r, k, 0:2, :])
        s = jnp.zeros_like(m)
        for k in range(n):
            s = s + buf[r, k, 2:4, :] * jnp.exp(buf[r, k, 0:2, :] - m)
        return m, s

    plane = y * 4 + z

    def second_stats(r, copies):
        m, s = merged(SA, r, 8, copies)
        SB[r, plane, 0:2, :] = m
        SB[r, plane, 2:4, :] = s
        return spread(SB, r, plane, False)

    G, PK, LN = S["G"], S["PK"], S["LN"]

    def grads(r, copies):
        m, s = merged(SB, r, 16, copies)
        norm = m + jnp.log(s)
        for b in range(2):
            LN[r, b * 128 : b * 128 + 128, :] = to_col(norm[b : b + 1, :])

        def part(i, _):
            rows = pl.ds(pl.multiple_of(i * 32, 32), 32)
            v = L[r, rows, :]
            sp = SP[r, rows, :]
            mass = jnp.sum(IP[i, r * 32 : r * 32 + 32, 0:TOP], axis=1, keepdims=True)
            G[r, rows, :] = (mass * jnp.exp(v - LN[r, rows, :]) - sp).astype(BF16)
            PK[rows, :] = jnp.sum(sp * v, axis=1, keepdims=True)
            return 0

        lax.fori_loop(0, 8, part, 0)
        for b in range(2):
            S["QA"][r, me, b : b + 1, :] = to_row(PK[b * 128 : b * 128 + 128, :])

    PR, DS, DR = S["PR"], S["DS"], S["DR"]

    def second_dot(r, half):
        f0 = half * (D // 2)
        v = lax.dot_general(
            G[r], W[f0 : f0 + D // 2, :], (((1,), (1,)), ((), ())), preferred_element_type=F32
        )
        for i in range(8):
            PR[r, half * 8 + i] = v[:, i * Z : i * Z + Z]

        def cast(i, _):
            DS[r, half * 8 + i] = PR[r, half * 8 + i, pl.ds(pl.multiple_of(oc * 128, 128), 128), :].astype(BF16)
            return 0

        lax.fori_loop(0, 8, cast, 0)
        part = pl.ds(half * 8, 8)
        return send(DS.at[r, part], DR.at[r, part], c=oc)

    def place(order, yg, zg, xb):
        of = {"x": xb, "y": yg, "z": zg}
        return tuple(of[a] for a in order)

    def phase1(r, copies):
        for cp in copies:
            cp.wait_recv()

        def part(i, _):
            yg, zg = i // 4, i % 4
            for xb in range(4):
                mine = pl.ds(pl.multiple_of(c * 128 + xb * 32, 32), 32)
                v = PR[r, i, mine, :] + DR[r, i, xb * 32 : xb * 32 + 32, :].astype(F32)
                PR[r, i, mine, :] = v
                for k, (order, rows) in enumerate(COLOURS):
                    p, q, s = place(order, yg, zg, xb)
                    r0, n = rows[r]
                    S[f"T1{r}{k}"][p, q * 4 + s] = v[r0 : r0 + n].astype(BF16)
            return 0

        lax.fori_loop(0, 16, part, 0)
        res = []
        for k, (order, _) in enumerate(COLOURS):
            a = order[0]
            T, R = S[f"T1{r}{k}"], S[f"R1{r}{k}"]
            res.append([send(T.at[step(a, d)], R.at[d - 1], **{a: step(a, d)}) for d in (1, 3, 2)])
        return res

    def phase2(r, copies):
        res = []
        for k, (order, rows) in enumerate(COLOURS):
            for cp in copies[k]:
                cp.wait_recv()
            a, b, _ = order
            r0, n = rows[r]
            R, T = S[f"R1{r}{k}"], S[f"T2{r}{k}"]

            def part(i, _, order=order, r0=r0, n=n, R=R, T=T):
                at = dict(zip(order, (co[order[0]], i // 4, i % 4)))
                row = pl.ds(pl.multiple_of(c * 128 + at["x"] * 32 + r0, 8), n)
                v = PR[r, at["y"] * 4 + at["z"], row, :]
                for d in range(3):
                    v = v + R[d, i].astype(F32)
                T[i // 4, i % 4] = v.astype(T.dtype)
                return 0

            lax.fori_loop(0, 16, part, 0)
            R2 = S[f"R2{r}{k}"]
            res.append([send(T.at[step(b, d)], R2.at[d - 1], **{b: step(b, d)}) for d in (1, 3, 2)])
        return res

    def phase3(r, copies):
        res = []
        for k, (order, rows) in enumerate(COLOURS):
            for cp in copies[k]:
                cp.wait_recv()
            _, b, e = order
            T2, R2, T3, R3 = S[f"T2{r}{k}"], S[f"R2{r}{k}"], S[f"T3{r}{k}"], S[f"R3{r}{k}"]
            for s in range(4):
                v = T2[co[b], s].astype(F32)
                for d in range(3):
                    v = v + R2[d, s].astype(F32)
                T3[s] = v
            res.append([send(T3.at[step(e, d)], R3.at[d - 1], **{e: step(e, d)}) for d in (1, 3, 2)])
        return res

    def finish(r, copies, weight):
        for k, (order, rows) in enumerate(COLOURS):
            for cp in copies[k]:
                cp.wait_recv()
            r0, n = rows[r]
            T3, R3 = S[f"T3{r}{k}"], S[f"R3{r}{k}"]
            v = T3[co[order[2]]]
            for d in range(3):
                v = v + R3[d]
            lo = r * 32 + r0
            out[lo : lo + n, :] = weight[lo : lo + n, :] * v

    QA, QB = S["QA"], S["QB"]

    sparse(0, 0, 8)
    to_sibling(1)
    sparse(0, 8, 16)
    wcopy.wait()
    for d in range(4):
        Cn[0][d].wait_recv()
    first_dot(0)
    a0 = stats(0)
    for d in range(4):
        Cn[1][d].wait_recv()
    first_dot(1)
    b0 = second_stats(0, a0)
    a1 = stats(1)
    sparse(1, 0, 16)
    b1 = second_stats(1, a1)
    grads(0, b0)
    d0 = [second_dot(0, 0), second_dot(0, 1)]
    grads(1, b1)
    p0 = phase1(0, d0)
    d1 = [second_dot(1, 0), second_dot(1, 1)]
    qa = spread(QA, 0, me, True) + spread(QA, 1, me, True)
    p1 = phase1(1, d1)
    p0 = phase2(0, p0)
    for cp in qa:
        cp.wait_recv()
    for r in range(2):
        tot = QA[r, 0]
        for k in range(1, 8):
            tot = tot + QA[r, k]
        QB[r, plane] = tot
    qb = spread(QB, 0, plane, False) + spread(QB, 1, plane, False)
    p1 = phase2(1, p1)
    p0 = phase3(0, p0)
    p1 = phase3(1, p1)

    small = (
        lax.broadcasted_iota(jnp.int32, (64, 64), 0) == lax.broadcasted_iota(jnp.int32, (64, 64), 1)
    )
    weight = jnp.sum(jnp.where(small, jnp.broadcast_to(tw[...], (64, 64)), 0.0), axis=1, keepdims=True)
    for cp in qb:
        cp.wait_recv()
    for r in range(2):
        tot = QB[r, 0]
        for k in range(1, 16):
            tot = tot + QB[r, k]
        for b in range(2):
            PK[b * 128 : b * 128 + 128, :] = to_col(tot[b : b + 1, :])
        mine = pl.ds(pl.multiple_of(me * 32, 32), 32)
        q = pr[r * 32 : r * 32 + 32, :]
        mass = jnp.sum(q, axis=1, keepdims=True)
        S["DV"][r * 32 : r * 32 + 32, :] = (
            jnp.sum(q * jnp.log(q), axis=1, keepdims=True) - PK[mine, :] + mass * LN[r, mine, :]
        )
    dv[...] = jnp.sum(jnp.where(small, jnp.broadcast_to(S["DV"][...], (64, 64)), 0.0), axis=0, keepdims=True)
    finish(0, p0, weight)
    finish(1, p1, weight)
    for cp in sent:
        cp.wait_send()


def body(hidden, head_weight, teacher_ids, teacher_probs, token_weight):
    T, D = hidden.shape
    C = head_weight.shape[1]
    Z = D // 16
    V = pltpu.VMEM
    scratch = {
        "W": V((D, C), BF16), "H": V((2, 256, D), BF16), "IP": V((8, T, 128), F32),
        "SP": V((2, 256, C), F32), "L": V((2, 256, C), F32), "ST": V((256, 2), F32),
        "SA": V((2, 8, 8, 128), F32), "SB": V((2, 16, 8, 128), F32),
        "QA": V((2, 8, 8, 128), F32), "QB": V((2, 16, 8, 128), F32),
        "G": V((2, 256, C), BF16), "PK": V((256, 1), F32), "LN": V((2, 256, 1), F32),
        "DV": V((T, 1), F32),
        "PR": V((2, 16, 256, Z), F32), "DS": V((2, 16, 128, Z), BF16), "DR": V((2, 16, 128, Z), BF16),
    }
    for r in range(2):
        for k, (_, rows) in enumerate(COLOURS):
            n = rows[r][1]
            scratch[f"T1{r}{k}"] = V((4, 16, n, Z), BF16)
            scratch[f"R1{r}{k}"] = V((3, 16, n, Z), BF16)
            scratch[f"T2{r}{k}"] = V((4, 4, n, Z), WIRE2)
            scratch[f"R2{r}{k}"] = V((3, 4, n, Z), WIRE2)
            scratch[f"T3{r}{k}"] = V((4, n, Z), F32)
            scratch[f"R3{r}{k}"] = V((3, n, Z), F32)
    scratch["ss"] = pltpu.SemaphoreType.DMA((220,))
    scratch["rs"] = pltpu.SemaphoreType.DMA((220,))
    scratch["ws"] = pltpu.SemaphoreType.DMA
    vm = pl.BlockSpec(memory_space=pltpu.VMEM)
    grad, div = pl.pallas_call(
        functools.partial(kernel, names=tuple(scratch)),
        out_shape=(jax.ShapeDtypeStruct((T, Z), F32), jax.ShapeDtypeStruct((1, T), F32)),
        in_specs=[vm, pl.BlockSpec(memory_space=pl.ANY), vm, vm, vm],
        out_specs=(vm, vm),
        scratch_shapes=list(scratch.values()),
        compiler_params=pltpu.CompilerParams(
            collective_id=0, has_side_effects=True, vmem_limit_bytes=67043328
        ),
        name="distill",
    )(hidden, head_weight, teacher_ids, teacher_probs, token_weight.reshape(1, T))
    return div.reshape(T), grad


def solution(mesh):
    split = Mesh(mesh.devices.reshape(4, 2, 4, 4), ("x", "c", "y", "z"))
    placed = (P(DP, None), P(None, DP + VOCAB), P(DP, None), P(DP, None), P(DP))
    return jax.shard_map(
        body, mesh=split, in_specs=placed, out_specs=(P(DP), P(DP, VOCAB)), check_vma=False
    )
```

time: 305 us -> 93.7 us (0.31)
  other arithmetic: 141 us -> 0 us
  Pallas kernels: 0 us -> 77.5 us
  waiting for transfers between devices: 64.6 us -> 0 us
  blocking collectives: 52.8 us -> 0 us
  matrix products: 19 us -> 0 us
  between operations: 14.2 us -> 0.64 us
  local copies, waits for them, and re-layouts: 4.42 us -> 15.2 us
  starting transfers between devices: 7.04 us -> 0 us
    reduce_sum x11 -> x0, other arithmetic: 132 us -> none  [the longest x8 131 us: add_group(): jnp.sum(jnp.where(matches, probs_part[:, :, None], 0.0), axis=1)]
    pallas_call x0 -> x1, Pallas kernels: none -> 77.5 us  [body(): pl.pallas_call(functools.partial(kernel, names=tuple(scratch)), out_shape...]
    all_gather x5 -> x0, blocking collectives: 52.8 us -> none  [the longest x4 39.5 us: all_in_one(): both, at, found = (lax.all_gather(jnp.concatenate(lines), axis), 0, {})]
    reduce_scatter x1 -> x0, waiting for transfers between devices: 47.5 us -> none  [body(): lax.psum_scatter(lax.dot_general(logit_grad, head_weight, (((1,), (1,)),...]
    dot_general x2 -> x0, matrix products: 19 us -> none  [the longest x1 10.7 us: body(): lax.dot_general(logit_grad, head_weight, (((1,), (1,)), ((), ())), prefer...]
    all_to_all x1 -> x0, waiting for transfers between devices: 16.4 us -> none  [sent_and_summed(): pieces = lax.all_to_all(split_up(x, dim, length), axis, 0, 0, tiled=True)]
    unnamed x4 -> x3, local copies, waits for them, and re-layouts: 0.23 us -> 15.2 us
    all_to_all x1 -> x0, starting transfers between devices: 6.96 us -> none  [sent_and_summed(): pieces = lax.all_to_all(split_up(x, dim, length), axis, 0, 0, tiled=True)]
  transfers between devices with their start and end apart: 3 -> 0, of which waited for: 2 -> 0; matrix products, arithmetic and copies ran while one was open for 46% -> 0% of each run, Pallas kernels for 0% -> 0%
where the time goes in v1:
time: 93.7 us; the launch traced here: 93.3 us
  Pallas kernels  77.5 us (83%)
  local copies, waits for them, and re-layouts  15.2 us (16%)
    pallas_call x1, Pallas kernels, body(): pl.pallas_call(functools.partial(kernel, names=tuple(scratch)), out_shape...  77.5 us
    unnamed x3, local copies, waits for them, and re-layouts  15.2 us

profile of v1, /device:TPU:0, one launch (start us, length us, event | category | flops | bytes accessed | tf_op | source)
XLA Modules:
  0.0 93.3 jit_solution(14711702010045549496)
XLA Ops:
  0.6 12.6 %copy.7.w = bf16[3584,1188]{1,0:T(8,128)(2,1)} copy(bf16[3584,1188]{0,1:T(8,128)(2,1)} %param.6) | data formatting | bytes 17031168 | tf_op args[1]
  13.2 77.5 %distill.1 = (f32[64,224]{1,0:T(8,128)}, f32[1,64]{1,0:T(1,128)}) custom-call(bf16[64,3584]{1,0:T(8,128)(2,1)} %h.1, bf16[3584,1188]{1,0:T(8,128)(2,1)} %copy.7.w, s32[64,64]{1,0:T(8,128)} %ids.1, f32[64,64]{1,0:T(8,128)} %pr.1, f32[1,64]{1,0:T(1,128)} %bitcast.2), custom_call_target="tpu_custom_call" | custom-call | tf_op jit(solution)/shard_map/distill/pallas_call | solution.py:423
  90.7 1.1 %copy.10 = f32[64]{0:T(128)} copy(f32[64]{0:T(128)} %bitcast.3) | data formatting | bytes 512
  91.8 1.5 %copy.11 = f32[64,224]{1,0:T(8,128)} copy(f32[64,224]{1,0:T(8,128)} %get-tuple-element.9) | data formatting | bytes 114688

commit v2 on v1

--- a/solution.py
+++ b/solution.py
@@ -24,7 +24,7 @@
 def kernel(h, w, ids, pr, tw, out, dv, *scratch, names):
     S = dict(zip(names, scratch))
     D = h.shape[1]
-    C = w.shape[1]
+    C = w.shape[0]
     TOP = ids.shape[1]
     Z = D // 16
     co = {a: lax.axis_index(a) for a in ("x", "c", "y", "z")}
@@ -178,7 +178,9 @@
         ]
 
     def first_dot(r):
-        L[r] = jnp.dot(H[r], W[...], preferred_element_type=F32)
+        L[r] = lax.dot_general(
+            H[r], W[...], (((1,), (1,)), ((), ())), preferred_element_type=F32
+        )
 
     def stats(r):
         def part(i, _):
@@ -239,9 +241,7 @@
 
     def second_dot(r, half):
         f0 = half * (D // 2)
-        v = lax.dot_general(
-            G[r], W[f0 : f0 + D // 2, :], (((1,), (1,)), ((), ())), preferred_element_type=F32
-        )
+        v = jnp.dot(G[r], W[:, f0 : f0 + D // 2], preferred_element_type=F32)
         for i in range(8):
             PR[r, half * 8 + i] = v[:, i * Z : i * Z + Z]
 
@@ -399,7 +399,7 @@
     Z = D // 16
     V = pltpu.VMEM
     scratch = {
-        "W": V((D, C), BF16), "H": V((2, 256, D), BF16), "IP": V((8, T, 128), F32),
+        "W": V((C, D), BF16), "H": V((2, 256, D), BF16), "IP": V((8, T, 128), F32),
         "SP": V((2, 256, C), F32), "L": V((2, 256, C), F32), "ST": V((256, 2), F32),
         "SA": V((2, 8, 8, 128), F32), "SB": V((2, 16, 8, 128), F32),
         "QA": V((2, 8, 8, 128), F32), "QB": V((2, 16, 8, 128), F32),
@@ -430,7 +430,7 @@
             collective_id=0, has_side_effects=True, vmem_limit_bytes=67043328
         ),
         name="distill",
-    )(hidden, head_weight, teacher_ids, teacher_probs, token_weight.reshape(1, T))
+    )(hidden, head_weight.T, teacher_ids, teacher_probs, token_weight.reshape(1, T))
     return div.reshape(T), grad
 
 

time: 93.7 us -> 80.9 us (0.86)
  local copies, waits for them, and re-layouts: 15.2 us -> 2.59 us
    unnamed x3 -> x2, local copies, waits for them, and re-layouts: 15.2 us -> 2.59 us
where the time goes in v2:
time: 80.9 us; the launch traced here: 80.7 us
  Pallas kernels  77.4 us (96%)
  local copies, waits for them, and re-layouts  2.59 us (3%)
    pallas_call x1, Pallas kernels, body(): pl.pallas_call(functools.partial(kernel, names=tuple(scratch)), out_shape...  77.4 us
    unnamed x2, local copies, waits for them, and re-layouts  2.59 us

profile of v2, /device:TPU:0, one launch (start us, length us, event | category | flops | bytes accessed | tf_op | source)
XLA Modules:
  0.0 80.7 jit_solution(6045259794835543016)
XLA Ops:
  0.6 77.4 %distill.1 = (f32[64,224]{1,0:T(8,128)}, f32[1,64]{1,0:T(1,128)}) custom-call(bf16[64,3584]{1,0:T(8,128)(2,1)} %h.1, bf16[1188,3584]{1,0:T(8,128)(2,1)} %bitcast.3, s32[64,64]{1,0:T(8,128)} %ids.1, f32[64,64]{1,0:T(8,128)} %pr.1, f32[1,64]{1,0:T(1,128)} %bitcast.4), custom_call_target="tpu_custom_call" | custom-call | tf_op jit(solution)/shard_map/distill/pallas_call | solution.py:423
  78.1 1.1 %copy.9 = f32[64]{0:T(128)} copy(f32[64]{0:T(128)} %bitcast.5) | data formatting | bytes 512
  79.2 1.5 %copy.10 = f32[64,224]{1,0:T(8,128)} copy(f32[64,224]{1,0:T(8,128)} %get-tuple-element.9) | data formatting | bytes 114688

commit v3 on v2

v3 whole, which is shorter than its diff:
```python
import functools

import jax
import jax.numpy as jnp
from jax import lax
from jax.experimental import pallas as pl
from jax.experimental.pallas import tpu as pltpu
from jax.sharding import Mesh
from jax.sharding import PartitionSpec as P

MESH = pl.DeviceIdType.MESH
DP = ("x", "c")
VOCAB = ("y", "z")
F32 = jnp.float32
BF16 = jnp.bfloat16
COLOURS = (
    (("x", "y", "z"), (((0, 0), (0, 1), (3, 0)), ((0, 0), (0, 1)))),
    (("y", "z", "x"), (((1, 0), (1, 1), (3, 1)), ((1, 0), (1, 1), (3, 0)))),
    (("z", "x", "y"), (((2, 0), (2, 1)), ((2, 0), (2, 1), (3, 1)))),
)


def kernel(h, w, ids_in, pr_in, tw_in, out, dv, *scratch, names):
    S = dict(zip(names, scratch))
    D = h.shape[1]
    C = w.shape[0]
    TOP = ids_in.shape[1]
    Z = D // 16
    co = {a: lax.axis_index(a) for a in ("x", "c", "y", "z")}
    x, c, y, z = co["x"], co["c"], co["y"], co["z"]
    oc = 1 - c
    count = [0]

    def step(axis, d):
        return lax.rem(co[axis] + d, 4)

    def send(src, dst, **dev):
        i = count[0]
        count[0] += 1
        cp = pltpu.make_async_remote_copy(
            src_ref=src, dst_ref=dst, send_sem=S["ss"].at[i], recv_sem=S["rs"].at[i],
            device_id=dev, device_id_type=MESH,
        )
        cp.start()
        sent.append(cp)
        return cp

    sent = []
    bar = pltpu.get_barrier_semaphore()
    for d in range(4):
        for e in range(2):
            if d or e:
                pl.semaphore_signal(
                    bar, inc=1, device_id={"x": step("x", d), "c": lax.rem(c + e, 2)}, device_id_type=MESH
                )
    for d in range(4):
        for e in range(4):
            if d or e:
                pl.semaphore_signal(
                    bar, inc=1, device_id={"y": step("y", d), "z": step("z", e)}, device_id_type=MESH
                )
    H, IP, W = S["H"], S["IP"], S["W"]
    me = c * 4 + x
    own = pl.ds(pl.multiple_of(me * 32, 32), 32)
    ids, pr, tw = S["ids"], S["pr"], S["tw"]
    local = [
        pltpu.make_async_copy(ids_in, ids, S["ls"].at[0]),
        pltpu.make_async_copy(pr_in, pr, S["ls"].at[1]),
        pltpu.make_async_copy(h.at[0:32, :], H.at[0, own, :], S["ls"].at[2]),
        pltpu.make_async_copy(h.at[32:64, :], H.at[1, own, :], S["ls"].at[3]),
        pltpu.make_async_copy(w, W, S["ls"].at[4]),
        pltpu.make_async_copy(tw_in, tw, S["ls"].at[5]),
    ]
    for cp in local:
        cp.start()
    for cp in local[:2]:
        cp.wait()
    IP[me, :, 0:TOP] = pr[...]
    IP[me, :, TOP : 2 * TOP] = ids[...].astype(F32)
    for cp in local[2:4]:
        cp.wait()
    pl.semaphore_wait(bar, 22)

    share = (lax.rem(y + 2 * z, 4), lax.rem(2 * y + z, 4))
    X, Pn, Cn, In, Ic = [{}, {}], [{}, {}], [{}, {}], {}, {}

    def hrows(r, core, xb, off, n):
        return H.at[r, pl.ds(pl.multiple_of(core * 128 + xb * 32 + off, 8), n), :]

    def send_x(r):
        for d in (1, 3, 2):
            part = hrows(r, c, x, share[r] * 8, 8)
            X[r][d] = send(part, part, x=step("x", d))
        whole = hrows(r, c, x, 0, 32)
        Cn[r][0] = send(whole, whole, c=oc)

    def forward(r):
        full, half = (("y", "z"), ("z", "y"))[r]
        for d in (1, 3, 2):
            X[r][d].wait_recv()
            xs = step("x", 4 - d)
            rows = pl.ds(pl.multiple_of(c * 128 + xs * 32 + share[r] * 8, 8), 8)
            whole = H.at[r, rows, :]
            lo, hi = H.at[r, rows, 0 : D // 2], H.at[r, rows, D // 2 : D]
            Pn[r][d] = [
                send(whole, whole, **{full: step(full, 1)}),
                send(whole, whole, **{full: step(full, 3)}),
                send(lo, lo, **{half: step(half, 1)}),
                send(hi, hi, **{half: step(half, 3)}),
            ]

    def to_sibling(r):
        for d in (1, 3, 2):
            for cp in Pn[r][d]:
                cp.wait_recv()
            xs = step("x", 4 - d)
            blk = hrows(r, c, xs, 0, 32)
            Cn[r][d] = send(blk, blk, c=oc)

    dp_index = x * 2 + c
    offset = (dp_index * 16 + y * 4 + z) * C
    SP = S["SP"]

    def sparse(r, lo, hi):
        def group(g, _):
            blk = g // 2
            j0 = r * 32 + (g % 2) * 16
            rows = pl.ds(pl.multiple_of(j0, 16), 16)
            local = IP[blk, rows, TOP : 2 * TOP].astype(jnp.int32) - offset
            local = jnp.where((local >= 0) & (local < C), local, -1).astype(jnp.int16)
            lane = lax.broadcasted_iota(jnp.int32, (16, 128), 1)
            n = -(-C // 128)
            cols = [(lane + 128 * k).astype(jnp.int16) for k in range(n)]
            acc = [jnp.full((16, 128), 127, jnp.int16) for _ in range(n)]
            for k in range(TOP):
                one = jnp.broadcast_to(local[:, k : k + 1], (16, 128))
                for j in range(n):
                    acc[j] = jnp.where(one == cols[j], jnp.int16(k), acc[j])
            for j in range(n):
                which = acc[j].astype(jnp.int32)
                wide = min(128, C - 128 * j)
                for s in range(2):
                    table = IP[blk, pl.ds(pl.multiple_of(j0 + s * 8, 8), 8), :]
                    sel = which[s * 8 : s * 8 + 8]
                    got = jnp.where(sel < TOP, jnp.take_along_axis(table, sel, axis=1), 0.0)
                    SP[r, pl.ds(pl.multiple_of(g * 16 + s * 8, 8), 8), 128 * j : 128 * j + wide] = got[:, :wide]
            return 0

        lax.fori_loop(lo, hi, group, 0)

    eye = (
        lax.broadcasted_iota(jnp.int32, (128, 128), 0) == lax.broadcasted_iota(jnp.int32, (128, 128), 1)
    )

    def to_row(col):
        return jnp.sum(jnp.where(eye, jnp.broadcast_to(col, (128, 128)), 0.0), axis=0, keepdims=True)

    def to_col(row):
        return jnp.sum(jnp.where(eye, jnp.broadcast_to(row, (128, 128)), 0.0), axis=1, keepdims=True)

    L, ST = S["L"], S["ST"]
    SA, SB = S["SA"], S["SB"]

    def spread(ref, near):
        if near:
            return [
                send(ref, ref, x=step("x", d), c=lax.rem(c + e, 2))
                for d in range(4) for e in range(2) if d or e
            ]
        return [
            send(ref, ref, y=step("y", d), z=step("z", e))
            for d in range(4) for e in range(4) if d or e
        ]

    def first_dot(r):
        L[r] = lax.dot_general(
            H[r], W[...], (((1,), (1,)), ((), ())), preferred_element_type=F32
        )

    def stats(r):
        def part(i, _):
            rows = pl.ds(pl.multiple_of(i * 32, 32), 32)
            v = L[r, rows, :]
            m = jnp.max(v, axis=1, keepdims=True)
            ST[rows, 0:1] = m
            ST[rows, 1:2] = jnp.sum(jnp.exp(v - m), axis=1, keepdims=True)
            return 0

        lax.fori_loop(0, 8, part, 0)
        for b in range(2):
            SA[r, me, b : b + 1, :] = to_row(ST[b * 128 : b * 128 + 128, 0:1])
            SA[r, me, b + 2 : b + 3, :] = to_row(ST[b * 128 : b * 128 + 128, 1:2])
        return spread(SA.at[r, me], True)

    def merged(buf, r, n, copies):
        for cp in copies:
            cp.wait_recv()
        m = buf[r, 0, 0:2, :]
        for k in range(1, n):
            m = jnp.maximum(m, buf[r, k, 0:2, :])
        s = jnp.zeros_like(m)
        for k in range(n):
            s = s + buf[r, k, 2:4, :] * jnp.exp(buf[r, k, 0:2, :] - m)
        return m, s

    plane = y * 4 + z

    def second_stats(r, copies):
        m, s = merged(SA, r, 8, copies)
        SB[r, plane, 0:2, :] = m
        SB[r, plane, 2:4, :] = s
        return spread(SB.at[r, plane], False)

    G, PK, LN, QA, QB = S["G"], S["PK"], S["LN"], S["QA"], S["QB"]

    def grads(r, copies):
        m, s = merged(SB, r, 16, copies)
        norm = m + jnp.log(s)
        for b in range(2):
            LN[r, b * 128 : b * 128 + 128, :] = to_col(norm[b : b + 1, :])

        def part(i, _):
            rows = pl.ds(pl.multiple_of(i * 32, 32), 32)
            v = L[r, rows, :]
            sp = SP[r, rows, :]
            mass = jnp.sum(IP[i, r * 32 : r * 32 + 32, 0:TOP], axis=1, keepdims=True)
            G[r, rows, :] = (mass * jnp.exp(v - LN[r, rows, :]) - sp).astype(BF16)
            PK[rows, :] = jnp.sum(sp * v, axis=1, keepdims=True)
            return 0

        lax.fori_loop(0, 8, part, 0)
        for b in range(2):
            QA[me, 2 * r + b : 2 * r + b + 1, :] = to_row(PK[b * 128 : b * 128 + 128, :])

    PR, DS, DR = S["PR"], S["DS"], S["DR"]

    def second_dot(r):
        v = jnp.dot(G[r, pl.ds(pl.multiple_of(oc * 128, 128), 128), :], W[...], preferred_element_type=F32)
        for i in range(16):
            DS[r, i, :, 0:Z] = v[:, i * Z : i * Z + Z].astype(BF16)
        cp = send(DS.at[r], DR.at[r], c=oc)
        v = jnp.dot(G[r, pl.ds(pl.multiple_of(c * 128, 128), 128), :], W[...], preferred_element_type=F32)
        for i in range(16):
            PR[r, i, :, 0:Z] = v[:, i * Z : i * Z + Z]
        return cp

    def place(order, yg, zg, xb):
        of = {"x": xb, "y": yg, "z": zg}
        return tuple(of[a] for a in order)

    def phase1(r, copy):
        copy.wait_recv()

        def part(i, _):
            yg, zg = i // 4, i % 4
            for xb in range(4):
                rows = pl.ds(xb * 32, 32)
                v = PR[r, i, rows, :] + DR[r, i, rows, :].astype(F32)
                PR[r, i, rows, :] = v
                for k, (order, tiles) in enumerate(COLOURS):
                    p, q, s = place(order, yg, zg, xb)
                    for t, (rb, lt) in enumerate(tiles[r]):
                        S[f"T1{r}{k}"][p, q * 4 + s, t] = v[rb * 8 : rb * 8 + 8, lt * 128 : lt * 128 + 128].astype(BF16)
            return 0

        lax.fori_loop(0, 16, part, 0)
        res = []
        for k, (order, _) in enumerate(COLOURS):
            a = order[0]
            T, R = S[f"T1{r}{k}"], S[f"R1{r}{k}"]
            res.append([send(T.at[step(a, d)], R.at[d - 1], **{a: step(a, d)}) for d in (1, 3, 2)])
        return res

    def phase2(r, copies):
        res = []
        for k, (order, tiles) in enumerate(COLOURS):
            for cp in copies[k]:
                cp.wait_recv()
            a, b, e = order
            R, T = S[f"R1{r}{k}"], S[f"T2{r}{k}"]

            def part(i, _, order=order, tiles=tiles[r], R=R, T=T):
                at = dict(zip(order, (co[order[0]], i // 4, i % 4)))
                for t, (rb, lt) in enumerate(tiles):
                    rows = pl.ds(pl.multiple_of(at["x"] * 32 + rb * 8, 8), 8)
                    v = PR[r, at["y"] * 4 + at["z"], rows, lt * 128 : lt * 128 + 128]
                    for d in range(3):
                        v = v + R[d, i, t].astype(F32)
                    T[i, t] = v.astype(BF16)
                return 0

            lax.fori_loop(0, 16, part, 0)
            R2 = S[f"R2{r}{k}"]
            res.append([
                send(T.at[step(b, d) * 4 + step(e, f)], R2.at[d * 4 + f - 1], **{b: step(b, d), e: step(e, f)})
                for d in range(4) for f in range(4) if d or f
            ])
        return res

    def finish(r, copies, weight):
        for k, (order, tiles) in enumerate(COLOURS):
            for cp in copies[k]:
                cp.wait_recv()
            _, b, e = order
            T2, R2 = S[f"T2{r}{k}"], S[f"R2{r}{k}"]
            for t, (rb, lt) in enumerate(tiles[r]):
                v = T2[co[b] * 4 + co[e], t].astype(F32)
                for j in range(15):
                    v = v + R2[j, t].astype(F32)
                lo, wide = r * 32 + rb * 8, min(128, Z - lt * 128)
                out[lo : lo + 8, lt * 128 : lt * 128 + wide] = weight[lo : lo + 8, :] * v[:, :wide]

    for d in (1, 3, 2):
        In[d] = send(IP.at[me], IP.at[me], x=step("x", d))
    send_x(0)
    send_x(1)
    Ic[0] = send(IP.at[me], IP.at[me], c=oc)
    for d in (1, 3, 2):
        In[d].wait_recv()
        s = c * 4 + step("x", 4 - d)
        Ic[d] = send(IP.at[s], IP.at[s], c=oc)
    for d in range(4):
        Ic[d].wait_recv()
    sparse(0, 0, 2)
    forward(0)
    sparse(0, 2, 8)
    forward(1)
    sparse(0, 8, 12)
    to_sibling(0)
    sparse(0, 12, 16)
    local[4].wait()
    for d in range(4):
        Cn[0][d].wait_recv()
    first_dot(0)
    to_sibling(1)
    a0 = stats(0)
    for d in range(4):
        Cn[1][d].wait_recv()
    first_dot(1)
    b0 = second_stats(0, a0)
    a1 = stats(1)
    sparse(1, 0, 8)
    b1 = second_stats(1, a1)
    sparse(1, 8, 16)
    grads(0, b0)
    p0 = second_dot(0)
    grads(1, b1)
    p0 = phase1(0, p0)
    p1 = second_dot(1)
    p1 = phase1(1, p1)
    qa = spread(QA.at[me], True)
    p0 = phase2(0, p0)
    for cp in qa:
        cp.wait_recv()
    tot = QA[0]
    for k in range(1, 8):
        tot = tot + QA[k]
    QB[plane] = tot
    qb = spread(QB.at[plane], False)
    p1 = phase2(1, p1)

    local[5].wait()
    small = (
        lax.broadcasted_iota(jnp.int32, (64, 64), 0) == lax.broadcasted_iota(jnp.int32, (64, 64), 1)
    )
    weight = jnp.sum(jnp.where(small, jnp.broadcast_to(tw[...], (64, 64)), 0.0), axis=1, keepdims=True)
    for cp in qb:
        cp.wait_recv()
    tot = QB[0]
    for k in range(1, 16):
        tot = tot + QB[k]
    for r in range(2):
        for b in range(2):
            PK[b * 128 : b * 128 + 128, :] = to_col(tot[2 * r + b : 2 * r + b + 1, :])
        q = pr[r * 32 : r * 32 + 32, :]
        mass = jnp.sum(q, axis=1, keepdims=True)
        S["DV"][r * 32 : r * 32 + 32, :] = (
            jnp.sum(q * jnp.log(q), axis=1, keepdims=True) - PK[own, :] + mass * LN[r, own, :]
        )
    dv[...] = jnp.sum(jnp.where(small, jnp.broadcast_to(S["DV"][...], (64, 64)), 0.0), axis=0, keepdims=True)
    finish(0, p0, weight)
    finish(1, p1, weight)
    for cp in sent:
        cp.wait_send()


def body(hidden, head_weight, teacher_ids, teacher_probs, token_weight):
    T, D = hidden.shape
    C = head_weight.shape[1]
    Z = D // 16
    V = pltpu.VMEM
    scratch = {
        "W": V((C, D), BF16), "H": V((2, 256, D), BF16), "IP": V((8, T, 128), F32),
        "SP": V((2, 256, C), F32), "L": V((2, 256, C), F32), "ST": V((256, 2), F32),
        "SA": V((2, 8, 8, 128), F32), "SB": V((2, 16, 8, 128), F32),
        "QA": V((8, 8, 128), F32), "QB": V((16, 8, 128), F32),
        "G": V((2, 256, C), BF16), "PK": V((256, 1), F32), "LN": V((2, 256, 1), F32),
        "DV": V((T, 1), F32),
        "PR": V((2, 16, 128, 256), F32), "DS": V((2, 16, 128, 256), BF16), "DR": V((2, 16, 128, 256), BF16),
        "ids": V(teacher_ids.shape, jnp.int32), "pr": V(teacher_probs.shape, F32), "tw": V((1, T), F32),
    }
    for r in range(2):
        for k, (_, tiles) in enumerate(COLOURS):
            n = len(tiles[r])
            scratch[f"T1{r}{k}"] = V((4, 16, n, 8, 128), BF16)
            scratch[f"R1{r}{k}"] = V((3, 16, n, 8, 128), BF16)
            scratch[f"T2{r}{k}"] = V((16, n, 8, 128), BF16)
            scratch[f"R2{r}{k}"] = V((15, n, 8, 128), BF16)
    scratch["ss"] = pltpu.SemaphoreType.DMA((224,))
    scratch["rs"] = pltpu.SemaphoreType.DMA((224,))
    scratch["ls"] = pltpu.SemaphoreType.DMA((6,))
    vm = pl.BlockSpec(memory_space=pltpu.VMEM)
    grad, div = pl.pallas_call(
        functools.partial(kernel, names=tuple(scratch)),
        out_shape=(jax.ShapeDtypeStruct((T, Z), F32), jax.ShapeDtypeStruct((1, T), F32)),
        in_specs=[pl.BlockSpec(memory_space=pl.ANY)] * 5,
        out_specs=(vm, vm),
        scratch_shapes=list(scratch.values()),
        compiler_params=pltpu.CompilerParams(
            collective_id=0, has_side_effects=True, vmem_limit_bytes=67043328
        ),
        name="distill",
    )(hidden, head_weight.T, teacher_ids, teacher_probs, token_weight.reshape(1, T))
    return div.reshape(T), grad


def solution(mesh):
    split = Mesh(mesh.devices.reshape(4, 2, 4, 4), ("x", "c", "y", "z"))
    placed = (P(DP, None), P(None, DP + VOCAB), P(DP, None), P(DP, None), P(DP))
    return jax.shard_map(
        body, mesh=split, in_specs=placed, out_specs=(P(DP), P(DP, VOCAB)), check_vma=False
    )
```

time: 80.9 us -> 70.8 us (0.88)
  Pallas kernels: 77.4 us -> 67.4 us
    pallas_call x1, Pallas kernels: 77.4 us -> 67.4 us  [body(): pl.pallas_call(functools.partial(kernel, names=tuple(scratch)), out_shape...]
where the time goes in v3:
time: 70.8 us; the launch traced here: 70.6 us
  Pallas kernels  67.4 us (95%)
  local copies, waits for them, and re-layouts  2.59 us (4%)
    pallas_call x1, Pallas kernels, body(): pl.pallas_call(functools.partial(kernel, names=tuple(scratch)), out_shape...  67.4 us
    unnamed x2, local copies, waits for them, and re-layouts  2.59 us

profile of v3, /device:TPU:0, one launch (start us, length us, event | category | flops | bytes accessed | tf_op | source)
XLA Modules:
  0.0 70.6 jit_solution(8598595943197063518)
XLA Ops:
  0.6 67.4 %distill.1 = (f32[64,224]{1,0:T(8,128)}, f32[1,64]{1,0:T(1,128)}) custom-call(bf16[64,3584]{1,0:T(8,128)(2,1)} %h.1, bf16[1188,3584]{1,0:T(8,128)(2,1)} %bitcast.3, s32[64,64]{1,0:T(8,128)} %ids_in.1, f32[64,64]{1,0:T(8,128)} %pr_in.1, f32[1,64]{1,0:T(1,128)} %bitcast.4), custom_call_target="tpu_custom_call" | custom-call | tf_op jit(solution)/shard_map/distill/pallas_call | solution.py:413
  68.0 1.1 %copy.9 = f32[64]{0:T(128)} copy(f32[64]{0:T(128)} %bitcast.5) | data formatting | bytes 512
  69.1 1.5 %copy.10 = f32[64,224]{1,0:T(8,128)} copy(f32[64,224]{1,0:T(8,128)} %get-tuple-element.9) | data formatting | bytes 114688

commit v4 on v3

--- a/solution.py
+++ b/solution.py
@@ -53,12 +53,9 @@
                 pl.semaphore_signal(
                     bar, inc=1, device_id={"x": step("x", d), "c": lax.rem(c + e, 2)}, device_id_type=MESH
                 )
-    for d in range(4):
-        for e in range(4):
-            if d or e:
-                pl.semaphore_signal(
-                    bar, inc=1, device_id={"y": step("y", d), "z": step("z", e)}, device_id_type=MESH
-                )
+    beside = [{"y": step("y", 1)}, {"y": step("y", 3)}, {"z": step("z", 1)}, {"z": step("z", 3)}]
+    for dev in beside:
+        pl.semaphore_signal(bar, inc=1, device_id=dev, device_id_type=MESH)
     H, IP, W = S["H"], S["IP"], S["W"]
     me = c * 4 + x
     own = pl.ds(pl.multiple_of(me * 32, 32), 32)
@@ -79,7 +76,14 @@
     IP[me, :, TOP : 2 * TOP] = ids[...].astype(F32)
     for cp in local[2:4]:
         cp.wait()
-    pl.semaphore_wait(bar, 22)
+    pl.semaphore_wait(bar, 11)
+
+    def tell(i):
+        for dev in beside:
+            pl.semaphore_signal(S["hs"].at[i], inc=1, device_id=dev, device_id_type=MESH)
+
+    def hear(i):
+        pl.semaphore_wait(S["hs"].at[i], 4)
 
     share = (lax.rem(y + 2 * z, 4), lax.rem(2 * y + z, 4))
     X, Pn, Cn, In, Ic = [{}, {}], [{}, {}], [{}, {}], {}, {}
@@ -89,25 +93,31 @@
 
     def send_x(r):
         for d in (1, 3, 2):
-            part = hrows(r, c, x, share[r] * 8, 8)
-            X[r][d] = send(part, part, x=step("x", d))
+            X[r][d] = []
+            for half in range(2):
+                rows = pl.ds(pl.multiple_of(me * 32 + share[half] * 8, 8), 8)
+                part = H.at[r, rows, half * (D // 2) : (half + 1) * (D // 2)]
+                X[r][d].append(send(part, part, x=step("x", d)))
         whole = hrows(r, c, x, 0, 32)
         Cn[r][0] = send(whole, whole, c=oc)
 
     def forward(r):
-        full, half = (("y", "z"), ("z", "y"))[r]
         for d in (1, 3, 2):
-            X[r][d].wait_recv()
             xs = step("x", 4 - d)
-            rows = pl.ds(pl.multiple_of(c * 128 + xs * 32 + share[r] * 8, 8), 8)
-            whole = H.at[r, rows, :]
-            lo, hi = H.at[r, rows, 0 : D // 2], H.at[r, rows, D // 2 : D]
-            Pn[r][d] = [
-                send(whole, whole, **{full: step(full, 1)}),
-                send(whole, whole, **{full: step(full, 3)}),
-                send(lo, lo, **{half: step(half, 1)}),
-                send(hi, hi, **{half: step(half, 3)}),
-            ]
+            Pn[r][d] = []
+            for half in range(2):
+                X[r][d][half].wait_recv()
+                more, less = (("y", "z"), ("z", "y"))[half]
+                rows = pl.ds(pl.multiple_of(c * 128 + xs * 32 + share[half] * 8, 8), 8)
+                at = half * (D // 2)
+                whole = H.at[r, rows, at : at + D // 2]
+                lo, hi = H.at[r, rows, at : at + D // 4], H.at[r, rows, at + D // 4 : at + D // 2]
+                Pn[r][d] += [
+                    send(whole, whole, **{more: step(more, 1)}),
+                    send(whole, whole, **{more: step(more, 3)}),
+                    send(lo, lo, **{less: step(less, 1)}),
+                    send(hi, hi, **{less: step(less, 3)}),
+                ]
 
     def to_sibling(r):
         for d in (1, 3, 2):
@@ -121,10 +131,10 @@
     offset = (dp_index * 16 + y * 4 + z) * C
     SP = S["SP"]
 
-    def sparse(r, lo, hi):
-        def group(g, _):
-            blk = g // 2
-            j0 = r * 32 + (g % 2) * 16
+    def sparse(r, blk):
+        def group(i, _):
+            g = blk * 2 + i
+            j0 = r * 32 + i * 16
             rows = pl.ds(pl.multiple_of(j0, 16), 16)
             local = IP[blk, rows, TOP : 2 * TOP].astype(jnp.int32) - offset
             local = jnp.where((local >= 0) & (local < C), local, -1).astype(jnp.int16)
@@ -146,7 +156,7 @@
                     SP[r, pl.ds(pl.multiple_of(g * 16 + s * 8, 8), 8), 128 * j : 128 * j + wide] = got[:, :wide]
             return 0
 
-        lax.fori_loop(lo, hi, group, 0)
+        lax.fori_loop(0, 2, group, 0)
 
     eye = (
         lax.broadcasted_iota(jnp.int32, (128, 128), 0) == lax.broadcasted_iota(jnp.int32, (128, 128), 1)
@@ -312,22 +322,38 @@
 
     for d in (1, 3, 2):
         In[d] = send(IP.at[me], IP.at[me], x=step("x", d))
+    Ic[0] = send(IP.at[me], IP.at[me], c=oc)
     send_x(0)
     send_x(1)
-    Ic[0] = send(IP.at[me], IP.at[me], c=oc)
+    tell(0)
+
+    def pair(r, d):
+        xs = step("x", 4 - d)
+        sparse(r, c * 4 + xs)
+        sparse(r, oc * 4 + xs)
+
+    sparse(0, me)
+    sparse(1, me)
+    Ic[0].wait_recv()
+    sparse(0, oc * 4 + x)
+    sparse(1, oc * 4 + x)
     for d in (1, 3, 2):
         In[d].wait_recv()
         s = c * 4 + step("x", 4 - d)
         Ic[d] = send(IP.at[s], IP.at[s], c=oc)
-    for d in range(4):
+    hear(0)
+    tell(1)
+    forward(0)
+    for d in (1, 3, 2):
         Ic[d].wait_recv()
-    sparse(0, 0, 2)
-    forward(0)
-    sparse(0, 2, 8)
+    pair(0, 1)
     forward(1)
-    sparse(0, 8, 12)
+    hear(1)
+    tell(2)
+    pair(0, 3)
+    pair(0, 2)
     to_sibling(0)
-    sparse(0, 12, 16)
+    pair(1, 1)
     local[4].wait()
     for d in range(4):
         Cn[0][d].wait_recv()
@@ -337,15 +363,16 @@
     for d in range(4):
         Cn[1][d].wait_recv()
     first_dot(1)
+    hear(2)
     b0 = second_stats(0, a0)
     a1 = stats(1)
-    sparse(1, 0, 8)
+    pair(1, 3)
+    pair(1, 2)
     b1 = second_stats(1, a1)
-    sparse(1, 8, 16)
     grads(0, b0)
     p0 = second_dot(0)
+    p0 = phase1(0, p0)
     grads(1, b1)
-    p0 = phase1(0, p0)
     p1 = second_dot(1)
     p1 = phase1(1, p1)
     qa = spread(QA.at[me], True)
@@ -384,6 +411,11 @@
         cp.wait_send()
 
 
+def hand_over(a, b, a_out, b_out):
+    a_out[...] = a[...]
+    b_out[...] = b[...]
+
+
 def body(hidden, head_weight, teacher_ids, teacher_probs, token_weight):
     T, D = hidden.shape
     C = head_weight.shape[1]
@@ -406,8 +438,9 @@
             scratch[f"R1{r}{k}"] = V((3, 16, n, 8, 128), BF16)
             scratch[f"T2{r}{k}"] = V((16, n, 8, 128), BF16)
             scratch[f"R2{r}{k}"] = V((15, n, 8, 128), BF16)
-    scratch["ss"] = pltpu.SemaphoreType.DMA((224,))
-    scratch["rs"] = pltpu.SemaphoreType.DMA((224,))
+    scratch["ss"] = pltpu.SemaphoreType.DMA((260,))
+    scratch["rs"] = pltpu.SemaphoreType.DMA((260,))
+    scratch["hs"] = pltpu.SemaphoreType.REGULAR((3,))
     scratch["ls"] = pltpu.SemaphoreType.DMA((6,))
     vm = pl.BlockSpec(memory_space=pltpu.VMEM)
     grad, div = pl.pallas_call(
@@ -421,6 +454,13 @@
         ),
         name="distill",
     )(hidden, head_weight.T, teacher_ids, teacher_probs, token_weight.reshape(1, T))
+    grad, div = pl.pallas_call(
+        hand_over,
+        out_shape=(jax.ShapeDtypeStruct((T, Z), F32), jax.ShapeDtypeStruct((1, T), F32)),
+        in_specs=[vm, vm],
+        out_specs=(vm, vm),
+        name="hand_over",
+    )(grad, div)
     return div.reshape(T), grad
 
 

time: 70.8 us -> 67 us (0.946)
  local copies, waits for them, and re-layouts: 2.59 us -> 0 us
  Pallas kernels: 67.4 us -> 66.2 us
    pallas_call x1, Pallas kernels: 67.4 us -> 64.7 us  [body(): pl.pallas_call(functools.partial(kernel, names=tuple(scratch)), out_shape...]
    unnamed x2 -> x0, local copies, waits for them, and re-layouts: 2.59 us -> none
    pallas_call x0 -> x1, Pallas kernels: none -> 1.48 us  [body(): pl.pallas_call(hand_over, out_shape=(jax.ShapeDtypeStruct((T, Z), F32), j...]
where the time goes in v4:
time: 67 us; the launch traced here: 66.8 us
  Pallas kernels  66.2 us (99%)
    pallas_call x1, Pallas kernels, body(): pl.pallas_call(functools.partial(kernel, names=tuple(scratch)), out_shape...  64.7 us
    pallas_call x1, Pallas kernels, body(): pl.pallas_call(hand_over, out_shape=(jax.ShapeDtypeStruct((T, Z), F32), j...  1.48 us

profile of v4, /device:TPU:0, one launch (start us, length us, event | category | flops | bytes accessed | tf_op | source)
XLA Modules:
  0.0 66.8 jit_solution(15984537574216980994)
XLA Ops:
  0.6 64.7 %distill.1 = (f32[64,224]{1,0:T(8,128)}, f32[1,64]{1,0:T(1,128)}) custom-call(bf16[64,3584]{1,0:T(8,128)(2,1)} %h.1, bf16[1188,3584]{1,0:T(8,128)(2,1)} %bitcast.3, s32[64,64]{1,0:T(8,128)} %ids_in.1, f32[64,64]{1,0:T(8,128)} %pr_in.1, f32[1,64]{1,0:T(1,128)} %bitcast.4), custom_call_target="tpu_custom_call" | custom-call | tf_op jit(solution)/shard_map/distill/pallas_call | solution.py:446
  65.3 1.5 %hand_over.1 = (f32[64,224]{1,0:T(8,128)}, f32[1,64]{1,0:T(1,128)}) custom-call(f32[64,224]{1,0:T(8,128)} %get-tuple-element.6.a, f32[1,64]{1,0:T(1,128)} %get-tuple-element.7.b), custom_call_target="tpu_custom_call" | custom-call | tf_op jit(solution)/shard_map/hand_over/pallas_call | solution.py:457

commit v5 on v4

--- a/solution.py
+++ b/solution.py
@@ -18,6 +18,9 @@
     (("y", "z", "x"), (((1, 0), (1, 1), (3, 1)), ((1, 0), (1, 1), (3, 0)))),
     (("z", "x", "y"), (((2, 0), (2, 1)), ((2, 0), (2, 1), (3, 1)))),
 )
+
+
+FAR_FIRST = sorted(((d, e) for d in range(4) for e in range(4) if d or e), key=lambda p: -sum(min(v, 4 - v) for v in p))
 
 
 def kernel(h, w, ids_in, pr_in, tw_in, out, dv, *scratch, names):
@@ -175,11 +178,11 @@
         if near:
             return [
                 send(ref, ref, x=step("x", d), c=lax.rem(c + e, 2))
-                for d in range(4) for e in range(2) if d or e
+                for d in (2, 1, 3, 0) for e in range(2) if d or e
             ]
         return [
             send(ref, ref, y=step("y", d), z=step("z", e))
-            for d in range(4) for e in range(4) if d or e
+            for d, e in FAR_FIRST
         ]
 
     def first_dot(r):
@@ -278,7 +281,7 @@
         for k, (order, _) in enumerate(COLOURS):
             a = order[0]
             T, R = S[f"T1{r}{k}"], S[f"R1{r}{k}"]
-            res.append([send(T.at[step(a, d)], R.at[d - 1], **{a: step(a, d)}) for d in (1, 3, 2)])
+            res.append([send(T.at[step(a, d)], R.at[d - 1], **{a: step(a, d)}) for d in (2, 1, 3)])
         return res
 
     def phase2(r, copies):
@@ -303,7 +306,7 @@
             R2 = S[f"R2{r}{k}"]
             res.append([
                 send(T.at[step(b, d) * 4 + step(e, f)], R2.at[d * 4 + f - 1], **{b: step(b, d), e: step(e, f)})
-                for d in range(4) for f in range(4) if d or f
+                for d, f in FAR_FIRST
             ])
         return res
 

time: 67 us -> 66.2 us (0.988)
  Pallas kernels: 66.2 us -> 65.2 us
    pallas_call x1, Pallas kernels: 64.7 us -> 63.8 us  [body(): pl.pallas_call(functools.partial(kernel, names=tuple(scratch)), out_shape...]
where the time goes in v5:
time: 66.2 us; the launch traced here: 65.9 us
  Pallas kernels  65.2 us (98%)
    pallas_call x1, Pallas kernels, body(): pl.pallas_call(functools.partial(kernel, names=tuple(scratch)), out_shape...  63.8 us
    pallas_call x1, Pallas kernels, body(): pl.pallas_call(hand_over, out_shape=(jax.ShapeDtypeStruct((T, Z), F32), j...  1.48 us

profile of v5, /device:TPU:0, one launch (start us, length us, event | category | flops | bytes accessed | tf_op | source)
XLA Modules:
  0.0 65.9 jit_solution(10772277895856038716)
XLA Ops:
  0.6 63.8 %distill.1 = (f32[64,224]{1,0:T(8,128)}, f32[1,64]{1,0:T(1,128)}) custom-call(bf16[64,3584]{1,0:T(8,128)(2,1)} %h.1, bf16[1188,3584]{1,0:T(8,128)(2,1)} %bitcast.3, s32[64,64]{1,0:T(8,128)} %ids_in.1, f32[64,64]{1,0:T(8,128)} %pr_in.1, f32[1,64]{1,0:T(1,128)} %bitcast.4), custom_call_target="tpu_custom_call" | custom-call | tf_op jit(solution)/shard_map/distill/pallas_call | solution.py:449
  64.4 1.5 %hand_over.1 = (f32[64,224]{1,0:T(8,128)}, f32[1,64]{1,0:T(1,128)}) custom-call(f32[64,224]{1,0:T(8,128)} %get-tuple-element.6.a, f32[1,64]{1,0:T(1,128)} %get-tuple-element.7.b), custom_call_target="tpu_custom_call" | custom-call | tf_op jit(solution)/shard_map/hand_over/pallas_call | solution.py:460

commit v6 on v5

--- a/solution.py
+++ b/solution.py
@@ -414,9 +414,12 @@
         cp.wait_send()
 
 
-def hand_over(a, b, a_out, b_out):
-    a_out[...] = a[...]
-    b_out[...] = b[...]
+def hand_over(a, b, a_out, b_out, sem):
+    copies = [pltpu.make_async_copy(a, a_out, sem.at[0]), pltpu.make_async_copy(b, b_out, sem.at[1])]
+    for cp in copies:
+        cp.start()
+    for cp in copies:
+        cp.wait()
 
 
 def body(hidden, head_weight, teacher_ids, teacher_probs, token_weight):
@@ -460,8 +463,9 @@
     grad, div = pl.pallas_call(
         hand_over,
         out_shape=(jax.ShapeDtypeStruct((T, Z), F32), jax.ShapeDtypeStruct((1, T), F32)),
-        in_specs=[vm, vm],
-        out_specs=(vm, vm),
+        in_specs=[pl.BlockSpec(memory_space=pl.ANY)] * 2,
+        out_specs=(pl.BlockSpec(memory_space=pl.ANY),) * 2,
+        scratch_shapes=[pltpu.SemaphoreType.DMA((2,))],
         name="hand_over",
     )(grad, div)
     return div.reshape(T), grad

time: 66.2 us -> 67.9 us (1.026)
  Pallas kernels: 65.2 us -> 66.9 us
    pallas_call x1, Pallas kernels: 1.48 us -> 3.12 us  [body(): pl.pallas_call(hand_over, out_shape=(jax.ShapeDtypeStruct((T, Z), F32), j...]
where the time goes in v6:
time: 67.9 us; the launch traced here: 67.7 us
  Pallas kernels  66.9 us (99%)
  between operations  0.8 us (1%)
    pallas_call x1, Pallas kernels, body(): pl.pallas_call(functools.partial(kernel, names=tuple(scratch)), out_shape...  63.8 us
    pallas_call x1, Pallas kernels, body(): pl.pallas_call(hand_over, out_shape=(jax.ShapeDtypeStruct((T, Z), F32), j...  3.12 us

profile of v6, /device:TPU:0, one launch (start us, length us, event | category | flops | bytes accessed | tf_op | source)
XLA Modules:
  0.0 67.7 jit_solution(7570340936130883129)
XLA Ops:
  0.6 63.8 %distill.1 = (f32[64,224]{1,0:T(8,128)}, f32[1,64]{1,0:T(1,128)}) custom-call(bf16[64,3584]{1,0:T(8,128)(2,1)} %h.1, bf16[1188,3584]{1,0:T(8,128)(2,1)} %bitcast.3, s32[64,64]{1,0:T(8,128)} %ids_in.1, f32[64,64]{1,0:T(8,128)} %pr_in.1, f32[1,64]{1,0:T(1,128)} %bitcast.4), custom_call_target="tpu_custom_call" | custom-call | tf_op jit(solution)/shard_map/distill/pallas_call | solution.py:452
  64.4 3.1 %hand_over.1 = (f32[64,224]{1,0:T(8,128)}, f32[1,64]{1,0:T(1,128)}) custom-call(f32[64,224]{1,0:T(8,128)} %get-tuple-element.6.a, f32[1,64]{1,0:T(1,128)} %get-tuple-element.7.b), custom_call_target="tpu_custom_call" | custom-call | tf_op jit(solution)/shard_map/hand_over/pallas_call | solution.py:463
